TPU v7x, 32 devices: a whole 2x2x4 slice. The times are simulated.
32 devices in a mesh: grp: 2 (over y), dev: 16 (over z, x, core).
Axes of the slice: x: 2, y: 2, z: 4, core: 2. Of those that a mesh axis runs over, the one named last changes fastest.
Arguments:
- pooled_grad: bfloat16 [4096, 32, 128], P(('grp', 'dev')), may hold values from -6 to 6
- row_ids: int32 [4096, 4, 32], P(('grp', 'dev')), may hold values from 0 to 1023
- scale_exps: int32 [4096, 32], P(('grp', 'dev')), may hold values from 0 to 3
- table_owner: int32 [32], replicated, may hold values from 0 to 31, each once
- dense_acts: bfloat16 [4096, 512], P(('grp', 'dev')), may hold values from -6 to 6
- dense_cot: bfloat16 [4096, 512], P(('grp', 'dev')), may hold values from -0.1875 to 0.1875
Outputs:
- table_grad: float32 [32, 1024, 128], P('dev')
- weight_grad: float32 [512, 512], replicated
- bias_grad: float32 [512], replicated
Inputs may be any that keep to these rules, and one draw needn't show every extreme that they name: Table t's rows are accumulated into slot table_owner[t]; each slot belongs to exactly one table.
All inputs are finite; a program needn't handle non-finite values.
Results may differ from a plain program's by a relative error of at most 0.0003.
Values may be sent and summed in bfloat16 or wider, within the bound.
A program may use at most 128 MiB of HBM per device.

v0:
```python
import math
import jax
import jax.numpy as jnp
from jax import lax
from jax.sharding import PartitionSpec as P

ROWS = 1024


def powers(exps):
    return (
        1.0
        + (exps >= 1).astype(jnp.float32)
        + 2.0 * (exps >= 2).astype(jnp.float32)
        + 4.0 * (exps >= 3).astype(jnp.float32)
    )


def accumulate(grads, indices, exps):
    samples = grads.shape[0]
    slots = grads.shape[2]
    pool_len = indices.shape[3]
    block_rows = math.gcd(samples, 1024)
    row_axis = lax.broadcasted_iota(jnp.int32, (ROWS, 1), 0)
    results = []
    for slot_pos in range(slots):
        factor = powers(exps[:, 0, slot_pos])
        restored = (grads[:, 0, slot_pos, :].astype(jnp.float32) * factor[:, None]).astype(
            jnp.bfloat16
        )
        row_index = indices[:, 0, slot_pos, :]

        def add_block(count, running, restored=restored, row_index=row_index):
            offset = count * block_rows
            values = lax.dynamic_slice_in_dim(restored, offset, block_rows, 0)
            picked = lax.dynamic_slice_in_dim(row_index, offset, block_rows, 0)
            counts = jnp.zeros((ROWS, block_rows), jnp.float32)
            for lookup in range(pool_len):
                counts = counts + (picked[:, lookup][None, :] == row_axis).astype(jnp.float32)
            return running + jnp.dot(
                counts.astype(jnp.bfloat16), values, preferred_element_type=jnp.float32
            )

        start_grad = jnp.zeros((ROWS, grads.shape[3]), jnp.float32)
        results.append(lax.fori_loop(0, samples // block_rows, add_block, start_grad))
    return jnp.stack(results, 0)


def per_device(pooled_grad, row_ids, scale_exps, table_owner, dense_acts, dense_cot):
    batch_rows, tables, feat_width = pooled_grad.shape
    dev_count = lax.axis_size("dev")
    per_owner = tables // dev_count
    pool_len = row_ids.shape[1]
    factor = powers(scale_exps)
    quantized = jnp.clip(pooled_grad.astype(jnp.float32) / factor[:, :, None], -1.0, 1.0).astype(
        jnp.bfloat16
    )
    slot_table = (
        jnp.zeros((tables,), jnp.int32).at[table_owner].set(jnp.arange(tables, dtype=jnp.int32))
    )
    send_grads = jnp.take(quantized, slot_table, axis=1).reshape(
        batch_rows, dev_count, per_owner, feat_width
    )
    send_rows = jnp.transpose(
        jnp.take(row_ids, slot_table, axis=2).reshape(batch_rows, pool_len, dev_count, per_owner),
        (0, 2, 3, 1),
    )
    send_exps = jnp.take(scale_exps, slot_table, axis=1).reshape(batch_rows, dev_count, per_owner)
    weight_term = lax.dot_general(
        dense_acts, dense_cot, (((0,), (0,)), ((), ())), preferred_element_type=jnp.float32
    )
    bias_term = jnp.sum(dense_cot.astype(jnp.float32), axis=0)
    partial_grad = accumulate(
        lax.all_to_all(send_grads, "dev", split_axis=1, concat_axis=0, tiled=True),
        lax.all_to_all(send_rows, "dev", split_axis=1, concat_axis=0, tiled=True),
        lax.all_to_all(send_exps, "dev", split_axis=1, concat_axis=0, tiled=True),
    )
    table_grad = lax.psum(partial_grad, "grp")
    dense_parts = (
        lax.psum_scatter(weight_term, "dev", scatter_dimension=0, tiled=True),
        lax.psum_scatter(bias_term, "dev", scatter_dimension=0, tiled=True),
    )
    dense_parts = lax.psum((dense_parts[0], dense_parts[1]), "grp")
    weight_grad, bias_grad = (
        lax.all_gather(dense_parts[0], "dev", axis=0, tiled=True),
        lax.all_gather(dense_parts[1], "dev", axis=0, tiled=True),
    )
    return (table_grad, weight_grad, bias_grad)


def solution(mesh):
    return jax.shard_map(
        per_device,
        mesh=mesh,
        in_specs=(
            P(("grp", "dev"), None, None),
            P(("grp", "dev"), None, None),
            P(("grp", "dev"), None),
            P(),
            P(("grp", "dev"), None),
            P(("grp", "dev"), None),
        ),
        out_specs=(P("dev", None, None), P(), P()),
        check_vma=False,
    )
```

profile of v0, /device:TPU:0, one launch (start us, length us, event | category | flops | bytes accessed | tf_op | source)
XLA Modules:
  0.0 227.3 jit_solution(12590961035273388617)
XLA Ops:
  7.2 0.7 compare_select_fusion.5
  7.9 0.7 scatter_custom_fusion
  8.7 1.3 gather_fusion.2
  10.0 0.7 broadcast_select_fusion.1
  10.7 7.4 %all-to-all-start.2 = ((s32[128,16,2]{0,2,1:T(2,128)}), s32[128,16,2]{0,2,1:T(2,128)S(1)}, u32[]{:S(2)}, u32[]{:S(2)}) async-start(s32[128,16,2]{0,2,1:T(2,128)} %broadcast_select_fusion.1), calls=%async_computation.2 | async-start | bytes 32768 | tf_op jit(solution)/shard_map/all_to_all | solution.py:76
  18.1 0.7 select_add_fusion
  18.8 0.6 gather_fusion
  20.1 1.4 clamp_convert_fusion
  21.5 0.7 fusion.14
  22.2 0.7 gather_fusion.1
  22.9 1.7 all-to-all-done.2
  24.6 4.4 %all-to-all-start = ((s32[128,16,2,4]{0,2,3,1:T(2,128)}), s32[128,16,2,4]{0,2,3,1:T(2,128)S(1)}, u32[]{:S(2)}, u32[]{:S(2)}) async-start(s32[128,16,2,4]{0,2,3,1:T(2,128)} %fusion.14), calls=%async_computation | async-start | bytes 131072 | tf_op jit(solution)/shard_map/all_to_all | solution.py:75
  29.0 1.1 broadcast_select_fusion
  30.1 5.8 %all-to-all-done = s32[128,16,2,4]{0,2,3,1:T(2,128)S(1)} async-done(((s32[128,16,2,4]{0,2,3,1:T(2,128)}), s32[128,16,2,4]{0,2,3,1:T(2,128)S(1)}, u32[]{:S(2)}, u32[]{:S(2)}) %all-to-all-start) | async-done | bytes 65568 | tf_op jit(solution)/shard_map/all_to_all | solution.py:75
  35.9 3.7 %all-to-all-start.1 = ((bf16[128,16,2,128]{3,0,2,1:T(8,128)(2,1)}), bf16[128,16,2,128]{3,0,2,1:T(8,128)(2,1)S(1)}, u32[]{:S(2)}, u32[]{:S(2)}) async-start(bf16[128,16,2,128]{3,0,2,1:T(8,128)(2,1)} %broadcast_select_fusion), calls=%async_computation.1 | async-start | bytes 2097152 | tf_op jit(solution)/shard_map/all_to_all | solution.py:74
  39.6 1.3 fusion.25
  41.1 21.3 %all-to-all-done.1 = bf16[128,16,2,128]{3,0,2,1:T(8,128)(2,1)S(1)} async-done(((bf16[128,16,2,128]{3,0,2,1:T(8,128)(2,1)}), bf16[128,16,2,128]{3,0,2,1:T(8,128)(2,1)S(1)}, u32[]{:S(2)}, u32[]{:S(2)}) %all-to-all-start.1) | async-done | bytes 1048608 | tf_op jit(solution)/shard_map/all_to_all | solution.py:74
  62.5 0.7 fusion.13
  63.2 4.5 %while.31 = (s32[]{:T(128)}, f32[1024,128]{1,0:T(8,128)S(1)}, s32[2048,4]{0,1:T(4,128)S(1)}, bf16[2048,128]{1,0:T(8,128)(2,1)S(1)}, s32[]{:T(128)}, /*index=5*/s...) while((s32[]{:T(128)}, f32[1024,128]{1,0:T(8,128)S(1)}, ...), condition=%wide.region_4.5_spmd.clone.clone, body=%wide.region_3.4_spmd.clone.clone.sunk | while | flops 281280512 | bytes 1360101 | solution.py:45
  63.4 2.1 fusion.35
  65.6 2.1 fusion.35
  67.7 4.5 %while.30 = (s32[]{:T(128)}, f32[1024,128]{1,0:T(8,128)S(1)}, s32[2048,4]{0,1:T(4,128)S(1)}, bf16[2048,128]{1,0:T(8,128)(2,1)S(1)}, s32[]{:T(128)}, /*index=5*/s...) while((s32[]{:T(128)}, f32[1024,128]{1,0:T(8,128)S(1)}, ...), condition=%wide.region_2.3_spmd.clone.clone, body=%wide.region_1.2_spmd.clone.clone.sunk | while | flops 281280512 | bytes 1360101 | solution.py:45
  67.8 2.1 fusion.33
  70.1 2.1 fusion.33
  72.2 1.0 pad_maximum_fusion
  73.2 30.2 %reduce-scatter.2.cloned.1.call-done = f32[32,512]{1,0:T(8,128)} async-done(((f32[512,512]{1,0:T(8,128)}), f32[32,512]{1,0:T(8,128)}) %reduce-scatter.2.cloned.1.call-update) | async-done | bytes 65552 | tf_op jit(solution)/shard_map/reduce_scatter | solution.py:80
  103.5 43.6 %all-reduce.5.cloned.1.call-done = (f32[2,1024,128]{2,1,0:T(8,128)}, f32[32,512]{1,0:T(8,128)}) async-done(((f32[2,1024,128]{2,1,0:T(8,128)}, f32[32,512]{1,0:T(8,128)}), (f32[2,1024,128]{2,1,0:T(8,128)}, f32[32,512]{1,0:T(8,128)})) %all-reduce.5.cloned.1.call-update) | async-done | bytes 1114128 | tf_op jit(solution)/shard_map/psum | solution.py:78
  148.4 33.2 %all-reduce.1 = f32[512]{0:T(512)S(1)} all-reduce(f32[512]{0:T(512)S(1)} %convert_reduce_fusion), channel_id=3, replica_groups=mesh['grp'=2,'dev'=16] {'dev'}, use_global_device_ids=true, to_apply=%region_9.10.clone | all-reduce | flops 512 | bytes 4096
  182.3 4.9 %psum.23 = f32[32]{0:T(128)S(1)} all-reduce(f32[32]{0:T(128)S(1)} %dynamic-slice.2), channel_id=1, replica_groups=mesh['grp'=2,'dev'=16] {'grp'}, use_global_device_ids=true, to_apply=%region_10.11 | all-reduce | flops 32 | bytes 256 | tf_op jit(solution)/shard_map/psum | solution.py:83
  187.4 30.0 %all-reduce = f32[512]{0:T(512)} all-reduce(f32[512]{0:T(512)S(1)} %dynamic-update-slice), channel_id=1, replica_groups=mesh['grp'=2,'dev'=16] {'dev'}, use_global_device_ids=true, to_apply=%add | all-reduce | flops 512 | bytes 4096
  217.5 2.4 %copy.52 = f32[2,1024,128]{2,1,0:T(8,128)} copy(f32[2,1024,128]{2,1,0:T(8,128)} %get-tuple-element.448) | data formatting | bytes 2097152
  219.8 1.0 copy.53
  (41 shorter events, 2.4 us)
Async XLA Ops:
  7.2 32.4 %copy-start = (bf16[128,512]{1,0:T(8,128)(2,1)S(1)}, bf16[128,512]{1,0:T(8,128)(2,1)}, u32[]{:S(2)}) copy-start(bf16[128,512]{1,0:T(8,128)(2,1)} %param.14) | copy-start | bytes 393220
  7.2 11.7 %copy-start.1 = (s32[128,4,32]{0,2,1:T(8,128)S(1)}, s32[128,4,32]{0,2,1:T(8,128)}, u32[]{:S(2)}) copy-start(s32[128,4,32]{0,2,1:T(8,128)} %param.11) | copy-start | bytes 196612
  10.7 13.9 %all-to-all-start.2 = ((s32[128,16,2]{0,2,1:T(2,128)}), s32[128,16,2]{0,2,1:T(2,128)S(1)}, u32[]{:S(2)}, u32[]{:S(2)}) async-start(s32[128,16,2]{0,2,1:T(2,128)} %broadcast_select_fusion.1), calls=%async_computation.2 | async-start | bytes 32768 | tf_op jit(solution)/shard_map/all_to_all | solution.py:76
  18.8 1.2 copy-start.2
  24.6 11.3 %all-to-all-start = ((s32[128,16,2,4]{0,2,3,1:T(2,128)}), s32[128,16,2,4]{0,2,3,1:T(2,128)S(1)}, u32[]{:S(2)}, u32[]{:S(2)}) async-start(s32[128,16,2,4]{0,2,3,1:T(2,128)} %fusion.14), calls=%async_computation | async-start | bytes 131072 | tf_op jit(solution)/shard_map/all_to_all | solution.py:75
  30.1 9.5 %copy-start.4 = (bf16[128,512]{1,0:T(8,128)(2,1)S(1)}, bf16[128,512]{1,0:T(8,128)(2,1)}, u32[]{:S(2)}) copy-start(bf16[128,512]{1,0:T(8,128)(2,1)} %param.15) | copy-start | bytes 393220
  35.9 26.5 %all-to-all-start.1 = ((bf16[128,16,2,128]{3,0,2,1:T(8,128)(2,1)}), bf16[128,16,2,128]{3,0,2,1:T(8,128)(2,1)S(1)}, u32[]{:S(2)}, u32[]{:S(2)}) async-start(bf16[128,16,2,128]{3,0,2,1:T(8,128)(2,1)} %broadcast_select_fusion), calls=%async_computation.1 | async-start | bytes 2097152 | tf_op jit(solution)/shard_map/all_to_all | solution.py:74
  39.5 63.9 %reduce-scatter.2.cloned.1.call-start = ((), (), s32[]{:S(2)}) async-start(), calls=%async_computation.4 | async-start | bytes 1114112 | tf_op jit(solution)/shard_map/reduce_scatter | solution.py:80
  40.9 106.2 %all-reduce.5.cloned.1.call-start = ((), (), s32[]{:S(2)}) async-start(), calls=%async_computation.6 | async-start | bytes 2228224 | tf_op jit(solution)/shard_map/psum | solution.py:78
  73.2 73.9 %copy-start.5 = (u32[32]{0:T(128)S(1)}, u32[32]{0:T(128)}, u32[]{:S(2)}) copy-start(u32[32]{0:T(128)} %constant.132) | copy-start | bytes 388
  103.5 114.0 %all-gather.2.cloned.1.call-start = ((), (), s32[]{:S(2)}) async-start(), calls=%async_computation.5 | async-start | bytes 1114112 | tf_op jit(solution)/shard_map/all_gather | solution.py:85
  217.5 2.4 %copy-start.3 = (f32[512,512]{1,0:T(8,128)S(1)}, f32[512,512]{1,0:T(8,128)}, u32[]{:S(2)}) copy-start(f32[512,512]{1,0:T(8,128)} %all-gather.2.cloned.1.call-done) | copy-start | bytes 3145732
Sparse Core Ops, SparseCore 0:
  44.6 58.8 reduce-scatter.1
  106.4 40.6 all-reduce.4
  149.3 37.8 all-gather.1
where the time goes:
time: 228 us; the launch traced here: 227 us
  waiting for transfers between devices  103 us (45%)
  blocking collectives  68.2 us (30%)
  starting transfers between devices  15.5 us (7%)
  between operations  15.3 us (7%)
  matrix products  9.65 us (4%)
  local copies, waits for them, and re-layouts  8.8 us (4%)
  other arithmetic  7.24 us (3%)
    unnamed x2, blocking collectives  63.2 us
    psum x1, waiting for transfers between devices, per_device(): table_grad = lax.psum(partial_grad, 'grp')  43.6 us
    reduce_scatter x1, waiting for transfers between devices, per_device(): lax.psum_scatter(weight_term, 'dev', scatter_dimension=0, tiled=True)  30.2 us
    all_to_all x1, waiting for transfers between devices, per_device(): lax.all_to_all(send_grads, 'dev', split_axis=1, concat_axis=0, tiled=True)  21.3 us
    dot_general x4, matrix products, add_block(): jnp.dot(counts.astype(jnp.bfloat16), values, preferred_element_type=jnp.f...  8.36 us
    all_to_all x1, starting transfers between devices, per_device(): lax.all_to_all(send_exps, 'dev', split_axis=1, concat_axis=0, tiled=True)  7.39 us
    all_to_all x1, waiting for transfers between devices, per_device(): lax.all_to_all(send_rows, 'dev', split_axis=1, concat_axis=0, tiled=True)  5.76 us
    psum x1, blocking collectives, per_device(): dense_parts = lax.psum((dense_parts[0], dense_parts[1]), 'grp')  4.93 us
  transfers between devices with their start and end apart: 6, of which 5 were waited for; matrix products, arithmetic and copies ran while one was open for 8% of the time, Pallas kernels for 0%

commit v1 on v0

--- a/solution.py
+++ b/solution.py
@@ -75,7 +75,7 @@
         lax.all_to_all(send_rows, "dev", split_axis=1, concat_axis=0, tiled=True),
         lax.all_to_all(send_exps, "dev", split_axis=1, concat_axis=0, tiled=True),
     )
-    table_grad = lax.psum(partial_grad, "grp")
+    table_grad = jnp.sum(lax.all_gather(partial_grad, "grp"), axis=0)
     dense_parts = (
         lax.psum_scatter(weight_term, "dev", scatter_dimension=0, tiled=True),
         lax.psum_scatter(bias_term, "dev", scatter_dimension=0, tiled=True),

time: 228 us -> 202 us (0.89)
  waiting for transfers between devices: 103 us -> 75.5 us
  local copies, waits for them, and re-layouts: 8.8 us -> 5.9 us
    psum x1, waiting for transfers between devices: 43.6 us -> 22.2 us  [per_device(): dense_parts = lax.psum((dense_parts[0], dense_parts[1]), 'grp')]
    all_to_all x1, waiting for transfers between devices: 21.3 us -> 0.01 us  [per_device(): lax.all_to_all(send_grads, 'dev', split_axis=1, concat_axis=0, tiled=True)]
    reduce_scatter x1, waiting for transfers between devices: 30.2 us -> 47 us  [per_device(): lax.psum_scatter(weight_term, 'dev', scatter_dimension=0, tiled=True)]
    unnamed x19 -> x20, local copies, waits for them, and re-layouts: 4.8 us -> 1.9 us
    reduce_sum x0 -> x1, other arithmetic: none -> 2.88 us  [per_device(): table_grad = jnp.sum(lax.all_gather(partial_grad, 'grp'), axis=0)]
  transfers between devices with their start and end apart: 6 -> 7, of which waited for: 5 -> 4; matrix products, arithmetic and copies ran while one was open for 8% -> 9% of each run, Pallas kernels for 0% -> 0%
where the time goes in v1:
time: 202 us; the launch traced here: 201 us
  waiting for transfers between devices  75.5 us (37%)
  blocking collectives  67.8 us (34%)
  starting transfers between devices  16.7 us (8%)
  between operations  15.4 us (8%)
  matrix products  10.6 us (5%)
  other arithmetic  9.41 us (5%)
  local copies, waits for them, and re-layouts  5.9 us (3%)
    unnamed x2, blocking collectives  62.9 us
    reduce_scatter x1, waiting for transfers between devices, per_device(): lax.psum_scatter(weight_term, 'dev', scatter_dimension=0, tiled=True)  47 us
    psum x1, waiting for transfers between devices, per_device(): dense_parts = lax.psum((dense_parts[0], dense_parts[1]), 'grp')  22.2 us
    dot_general x4, matrix products, add_block(): jnp.dot(counts.astype(jnp.bfloat16), values, preferred_element_type=jnp.f...  8.37 us
    all_to_all x1, starting transfers between devices, per_device(): lax.all_to_all(send_exps, 'dev', split_axis=1, concat_axis=0, tiled=True)  7.39 us
    all_to_all x1, waiting for transfers between devices, per_device(): lax.all_to_all(send_rows, 'dev', split_axis=1, concat_axis=0, tiled=True)  5.76 us
    all_to_all x1, starting transfers between devices, per_device(): lax.all_to_all(send_rows, 'dev', split_axis=1, concat_axis=0, tiled=True)  5.49 us
    psum x1, blocking collectives, per_device(): dense_parts = lax.psum((dense_parts[0], dense_parts[1]), 'grp')  4.93 us
  transfers between devices with their start and end apart: 7, of which 4 were waited for; matrix products, arithmetic and copies ran while one was open for 9% of the time, Pallas kernels for 0%

profile of v1, /device:TPU:0, one launch (start us, length us, event | category | flops | bytes accessed | tf_op | source)
XLA Modules:
  0.0 201.5 jit_solution(13847989534407465325)
XLA Ops:
  7.2 0.7 compare_select_fusion.5
  7.9 0.7 scatter_custom_fusion
  8.7 1.3 gather_fusion.2
  10.0 0.7 broadcast_select_fusion.1
  10.7 7.4 %all-to-all-start.2 = ((s32[128,16,2]{0,2,1:T(2,128)}), s32[128,16,2]{0,2,1:T(2,128)S(1)}, u32[]{:S(2)}, u32[]{:S(2)}) async-start(s32[128,16,2]{0,2,1:T(2,128)} %broadcast_select_fusion.1), calls=%async_computation.2 | async-start | bytes 32768 | tf_op jit(solution)/shard_map/all_to_all | solution.py:76
  18.2 2.3 %fusion.25 = f32[512,512]{1,0:T(8,128)} fusion(bf16[128,512]{1,0:T(8,128)(2,1)S(1)} %copy-done, bf16[128,512]{1,0:T(8,128)(2,1)} %param.15), kind=kOutput, calls=%fused_computation.62 | convolution fusion | flops 67108864 | bytes 1310720 | tf_op jit(solution)/shard_map/dot_general | solution.py:69
  20.5 0.6 gather_fusion
  21.2 1.4 clamp_convert_fusion
  22.6 0.7 fusion.14
  23.3 0.7 gather_fusion.1
  24.1 0.5 all-to-all-done.2
  24.6 5.5 %all-to-all-start = ((s32[128,16,2,4]{0,2,3,1:T(2,128)}), s32[128,16,2,4]{0,2,3,1:T(2,128)S(1)}, u32[]{:S(2)}, u32[]{:S(2)}) async-start(s32[128,16,2,4]{0,2,3,1:T(2,128)} %fusion.14), calls=%async_computation | async-start | bytes 131072 | tf_op jit(solution)/shard_map/all_to_all | solution.py:75
  30.1 1.1 broadcast_select_fusion
  31.2 5.8 %all-to-all-done = s32[128,16,2,4]{0,2,3,1:T(2,128)S(1)} async-done(((s32[128,16,2,4]{0,2,3,1:T(2,128)}), s32[128,16,2,4]{0,2,3,1:T(2,128)S(1)}, u32[]{:S(2)}, u32[]{:S(2)}) %all-to-all-start) | async-done | bytes 65568 | tf_op jit(solution)/shard_map/all_to_all | solution.py:75
  37.0 3.7 %all-to-all-start.1 = ((bf16[128,16,2,128]{3,0,2,1:T(8,128)(2,1)}), bf16[128,16,2,128]{3,0,2,1:T(8,128)(2,1)S(1)}, u32[]{:S(2)}, u32[]{:S(2)}) async-start(bf16[128,16,2,128]{3,0,2,1:T(8,128)(2,1)} %broadcast_select_fusion), calls=%async_computation.1 | async-start | bytes 2097152 | tf_op jit(solution)/shard_map/all_to_all | solution.py:74
  40.8 47.0 %reduce-scatter.2.cloned.1.call-done = f32[32,512]{1,0:T(8,128)} async-done(((f32[512,512]{1,0:T(8,128)}), f32[32,512]{1,0:T(8,128)}) %reduce-scatter.2.cloned.1.call-update) | async-done | bytes 65552 | tf_op jit(solution)/shard_map/reduce_scatter | solution.py:80
  87.9 22.2 %all-reduce.4.cloned.1.call-done = f32[32,512]{1,0:T(8,128)} async-done(((f32[32,512]{1,0:T(8,128)}), f32[32,512]{1,0:T(8,128)}) %all-reduce.4.cloned.1.call-update) | async-done | bytes 65552 | tf_op jit(solution)/shard_map/psum | solution.py:83
  110.3 0.7 fusion.13
  111.0 4.5 %while.31 = (s32[]{:T(128)}, f32[1024,128]{1,0:T(8,128)S(1)}, s32[2048,4]{0,1:T(4,128)S(1)}, bf16[2048,128]{1,0:T(8,128)(2,1)S(1)}, s32[]{:T(128)}, /*index=5*/s...) while((s32[]{:T(128)}, f32[1024,128]{1,0:T(8,128)S(1)}, ...), condition=%wide.region_4.5_spmd.clone.clone, body=%wide.region_3.4_spmd.clone.clone.sunk | while | flops 281280512 | bytes 1360101 | solution.py:45
  111.2 2.1 %fusion.35 = f32[1024,128]{1,0:T(8,128)S(1)} fusion(s32[1024]{0:T(1024)S(1)} %bitcast.83, s32[1024]{0:T(1024)S(1)} %bitcast.81, s32[1024]{0:T(1024)S(1)} %bitcast.82, s32[1024]{0:T(1024)S(1)} %bitcast.80, f32[1024,128]{1,0:T(8,128)S(1)} %get-tuple-element.389, bf16[2048,128]{1,0:T(8,128)(2,1)S(1)} %get-tuple-element.402, s32[]{:T(128)S(6)} %select_n.64, ...), kind=kOutput, calls=%fused_computation.22.clone.1 | convolution fusion | flops 281280512 | bytes 1327109 | tf_op jit(solution)/shard_map/while/body/eval_jaxpr/dot_general | solution.py:40
  113.4 2.1 %fusion.35 = f32[1024,128]{1,0:T(8,128)S(1)} fusion(s32[1024]{0:T(1024)S(1)} %bitcast.83, s32[1024]{0:T(1024)S(1)} %bitcast.81, s32[1024]{0:T(1024)S(1)} %bitcast.82, s32[1024]{0:T(1024)S(1)} %bitcast.80, f32[1024,128]{1,0:T(8,128)S(1)} %get-tuple-element.389, bf16[2048,128]{1,0:T(8,128)(2,1)S(1)} %get-tuple-element.402, s32[]{:T(128)S(6)} %select_n.64, ...), kind=kOutput, calls=%fused_computation.22.clone.1 | convolution fusion | flops 281280512 | bytes 1327109 | tf_op jit(solution)/shard_map/while/body/eval_jaxpr/dot_general | solution.py:40
  115.5 4.5 %while.30 = (s32[]{:T(128)}, f32[1024,128]{1,0:T(8,128)S(1)}, s32[2048,4]{0,1:T(4,128)S(1)}, bf16[2048,128]{1,0:T(8,128)(2,1)S(1)}, s32[]{:T(128)}, /*index=5*/s...) while((s32[]{:T(128)}, f32[1024,128]{1,0:T(8,128)S(1)}, ...), condition=%wide.region_2.3_spmd.clone.clone, body=%wide.region_1.2_spmd.clone.clone.sunk | while | flops 281280512 | bytes 1360101 | solution.py:45
  115.6 2.1 %fusion.33 = f32[1024,128]{1,0:T(8,128)S(1)} fusion(s32[1024]{0:T(1024)S(1)} %bitcast.87, s32[1024]{0:T(1024)S(1)} %bitcast.85, s32[1024]{0:T(1024)S(1)} %bitcast.86, s32[1024]{0:T(1024)S(1)} %bitcast.84, f32[1024,128]{1,0:T(8,128)S(1)} %get-tuple-element.422, bf16[2048,128]{1,0:T(8,128)(2,1)S(1)} %get-tuple-element.435, s32[]{:T(128)S(6)} %select_n.63, ...), kind=kOutput, calls=%fused_computation.12.clone.1 | convolution fusion | flops 281280512 | bytes 1327109 | tf_op jit(solution)/shard_map/while/body/eval_jaxpr/dot_general | solution.py:40
  117.9 2.1 %fusion.33 = f32[1024,128]{1,0:T(8,128)S(1)} fusion(s32[1024]{0:T(1024)S(1)} %bitcast.87, s32[1024]{0:T(1024)S(1)} %bitcast.85, s32[1024]{0:T(1024)S(1)} %bitcast.86, s32[1024]{0:T(1024)S(1)} %bitcast.84, f32[1024,128]{1,0:T(8,128)S(1)} %get-tuple-element.422, bf16[2048,128]{1,0:T(8,128)(2,1)S(1)} %get-tuple-element.435, s32[]{:T(128)S(6)} %select_n.63, ...), kind=kOutput, calls=%fused_computation.12.clone.1 | convolution fusion | flops 281280512 | bytes 1327109 | tf_op jit(solution)/shard_map/while/body/eval_jaxpr/dot_general | solution.py:40
  120.0 1.0 pad_maximum_fusion
  121.1 0.6 fusion.24
  122.4 32.8 %all-reduce.1 = f32[512]{0:T(512)S(1)} all-reduce(f32[512]{0:T(512)S(1)} %convert_reduce_fusion), channel_id=4, replica_groups=mesh['grp'=2,'dev'=16] {'dev'}, use_global_device_ids=true, to_apply=%region_9.10.clone | all-reduce | flops 512 | bytes 4096
  155.9 4.9 %psum.15 = f32[32]{0:T(128)S(1)} all-reduce(f32[32]{0:T(128)S(1)} %dynamic-slice.2), channel_id=1, replica_groups=mesh['grp'=2,'dev'=16] {'grp'}, use_global_device_ids=true, to_apply=%region_10.11 | all-reduce | flops 32 | bytes 256 | tf_op jit(solution)/shard_map/psum | solution.py:83
  160.9 0.2 dynamic-update-slice
  161.0 30.0 %all-reduce = f32[512]{0:T(512)} all-reduce(f32[512]{0:T(512)S(1)} %dynamic-update-slice), channel_id=1, replica_groups=mesh['grp'=2,'dev'=16] {'dev'}, use_global_device_ids=true, to_apply=%add | all-reduce | flops 512 | bytes 4096
  191.1 2.9 %reduce_sum.18 = f32[2,1024,128]{2,1,0:T(8,128)} reduce(f32[2,2,1024,128]{3,2,1,0:T(8,128)} %bitcast.74, f32[]{:T(128)} %constant.118.clone.1), dimensions={0}, to_apply=%region_5.6 | reduce | flops 262144 | bytes 3145732 | tf_op jit(solution)/shard_map/reduce_sum | solution.py:78
  194.0 1.0 copy.51
  (46 shorter events, 1.1 us)
Async XLA Ops:
  7.2 11.0 %copy-start = (bf16[128,512]{1,0:T(8,128)(2,1)S(1)}, bf16[128,512]{1,0:T(8,128)(2,1)}, u32[]{:S(2)}) copy-start(bf16[128,512]{1,0:T(8,128)(2,1)} %param.14) | copy-start | bytes 393220
  7.2 13.3 %copy-start.2 = (s32[128,32]{0,1:T(8,128)S(1)}, s32[128,32]{0,1:T(8,128)}, u32[]{:S(2)}) copy-start(s32[128,32]{0,1:T(8,128)} %param.12) | copy-start | bytes 49156
  7.2 13.3 %copy-start.1 = (s32[128,4,32]{0,2,1:T(8,128)S(1)}, s32[128,4,32]{0,2,1:T(8,128)}, u32[]{:S(2)}) copy-start(s32[128,4,32]{0,2,1:T(8,128)} %param.11) | copy-start | bytes 196612
  10.7 13.9 %all-to-all-start.2 = ((s32[128,16,2]{0,2,1:T(2,128)}), s32[128,16,2]{0,2,1:T(2,128)S(1)}, u32[]{:S(2)}, u32[]{:S(2)}) async-start(s32[128,16,2]{0,2,1:T(2,128)} %broadcast_select_fusion.1), calls=%async_computation.2 | async-start | bytes 32768 | tf_op jit(solution)/shard_map/all_to_all | solution.py:76
  18.1 3.1 %copy-start.3 = (bf16[128,32,128]{2,1,0:T(8,128)(2,1)S(1)}, bf16[128,32,128]{2,1,0:T(8,128)(2,1)}, u32[]{:S(2)}) copy-start(bf16[128,32,128]{2,1,0:T(8,128)(2,1)} %param.10) | copy-start | bytes 3145732
  18.1 69.7 %reduce-scatter.2.cloned.1.call-start = ((), (), s32[]{:S(2)}) async-start(), calls=%async_computation.4 | async-start | bytes 1114112 | tf_op jit(solution)/shard_map/reduce_scatter | solution.py:80
  24.6 12.4 %all-to-all-start = ((s32[128,16,2,4]{0,2,3,1:T(2,128)}), s32[128,16,2,4]{0,2,3,1:T(2,128)S(1)}, u32[]{:S(2)}, u32[]{:S(2)}) async-start(s32[128,16,2,4]{0,2,3,1:T(2,128)} %fusion.14), calls=%async_computation | async-start | bytes 131072 | tf_op jit(solution)/shard_map/all_to_all | solution.py:75
  37.0 73.2 %all-to-all-start.1 = ((bf16[128,16,2,128]{3,0,2,1:T(8,128)(2,1)}), bf16[128,16,2,128]{3,0,2,1:T(8,128)(2,1)S(1)}, u32[]{:S(2)}, u32[]{:S(2)}) async-start(bf16[128,16,2,128]{3,0,2,1:T(8,128)(2,1)} %broadcast_select_fusion), calls=%async_computation.1 | async-start | bytes 2097152 | tf_op jit(solution)/shard_map/all_to_all | solution.py:74
  40.7 69.4 %all-reduce.4.cloned.1.call-start = ((), (), s32[]{:S(2)}) async-start(), calls=%async_computation.5 | async-start | bytes 131072 | tf_op jit(solution)/shard_map/psum | solution.py:83
  87.8 103.3 %all-gather.4.cloned.1.call-start = ((), (), s32[]{:S(2)}) async-start(), calls=%async_computation.6 | async-start | bytes 1114112 | tf_op jit(solution)/shard_map/all_gather | solution.py:85
  110.1 81.0 %all-gather.6.cloned.1.call-start = ((), (), s32[]{:S(2)}) async-start(), calls=%async_computation.7 | async-start | bytes 3145728 | tf_op jit(solution)/shard_map/all_gather | solution.py:78
  120.0 1.1 copy-start.6
  120.0 2.3 %copy-start.5 = (bf16[128,512]{1,0:T(8,128)(2,1)S(1)}, bf16[128,512]{1,0:T(8,128)(2,1)}, u32[]{:S(2)}) copy-start(bf16[128,512]{1,0:T(8,128)(2,1)} %param.15) | copy-start | bytes 393220
  191.1 2.9 %copy-start.4 = (f32[512,512]{1,0:T(8,128)S(1)}, f32[512,512]{1,0:T(8,128)}, u32[]{:S(2)}) copy-start(f32[512,512]{1,0:T(8,128)} %all-gather.4.cloned.1.call-done) | copy-start | bytes 3145732
Sparse Core Ops, SparseCore 0:
  23.1 64.6 reduce-scatter.1
  90.0 20.0 all-reduce.3
  112.3 37.8 all-gather.3
  152.2 31.9 all-gather.5
